TPU v7x, 32 devices: a whole 2x2x4 slice. The times are simulated.
32 devices in a mesh: ep: 4 (over y, x), tp: 8 (over z, core).
Axes of the slice: x: 2, y: 2, z: 4, core: 2. Of those that a mesh axis runs over, the one named last changes fastest.
Arguments:
- tokens: bfloat16 [512, 6144], P('ep'), may hold values from -6 to 6
- expert_ids: int32 [512, 2], P('ep'), may hold values from 0 to 3, all different within a row; in each aligned block of 128 rows (0 to 127, 128 to 255, ...) at most 96 rows name the same one
- router: bfloat16 [6144, 4], replicated, may hold values from -0.078125 to 0.078125
- gate_weight: bfloat16 [4, 6144, 8192], P('ep', None, 'tp'), may hold values from -0.078125 to 0.078125
- up_weight: bfloat16 [4, 6144, 8192], P('ep', None, 'tp'), may hold values from -0.078125 to 0.078125
- down_weight: bfloat16 [4, 8192, 6144], P('ep', 'tp'), may hold values from -0.0625 to 0.0625
- keep_mask: int32 [512, 6144], P('ep'), may hold values 0 or 1
Outputs:
- layer_out: bfloat16 [512, 6144], P('ep')
Inputs may be any that keep to these rules, and one draw needn't show every extreme that they name: `expert_ids`: each row names two different experts. In the rows of one token block of 128 rows no expert is named more than 96 times, a bound that some block reaches.
All inputs are finite; a program needn't handle non-finite values. No bound on the sum of `keep_mask` on one device may be relied on, other than what follows from the above.
Results may differ from a plain program's by a relative error of at most 0.018.
Values may be sent and summed in bfloat16 or wider, within the bound.
A program may use at most 128 MiB of HBM per device.

v0:
```python
import jax
import jax.numpy as jnp
from jax import lax
from jax.sharding import PartitionSpec as P


def shards(tokens, expert_ids, router, gate_weight, up_weight, down_weight, keep_mask):
    experts = router.shape[1]
    tok_rows = tokens.shape[0]
    width_model = tokens.shape[1]
    capacity = 3 * tok_rows // experts
    groups = lax.axis_size("tp")
    share = capacity // groups
    logits = jnp.dot(tokens, router, preferred_element_type=jnp.float32)
    picked = jnp.take_along_axis(logits, expert_ids, axis=1)
    weight_first = jax.nn.sigmoid(picked[:, 0] - picked[:, 1])
    weight_second = jax.nn.sigmoid(picked[:, 1] - picked[:, 0])
    onehot = (expert_ids[:, :, None] == jnp.arange(experts, dtype=jnp.int32)[None, None, :]).astype(
        jnp.int32
    )
    onehot = onehot.reshape(tok_rows * 2, experts)
    ranks = jnp.cumsum(onehot, axis=0) - onehot
    slot = jnp.sum(ranks * onehot, axis=1).reshape(tok_rows, 2)
    place = slot * experts + expert_ids
    lines = jnp.arange(experts * capacity, dtype=jnp.int32)
    picker = ((place[None, :, 0] == lines[:, None]) | (place[None, :, 1] == lines[:, None])).astype(
        jnp.bfloat16
    )
    outgoing = jnp.dot(picker, tokens, preferred_element_type=jnp.float32).astype(jnp.bfloat16)
    outgoing = outgoing.reshape(capacity, experts, width_model)
    w_gate = gate_weight[0]
    w_up = up_weight[0]
    w_down = down_weight[0]
    arrived = lax.all_to_all(outgoing, "ep", split_axis=1, concat_axis=1, tiled=True)
    rows = arrived.reshape(capacity * experts, width_model)
    gate = jnp.dot(rows, w_gate, preferred_element_type=jnp.float32)
    up = jnp.dot(rows, w_up, preferred_element_type=jnp.float32)
    hidden = (jax.nn.silu(gate) * up).astype(jnp.bfloat16)
    summed = lax.psum_scatter(
        jnp.dot(hidden, w_down, preferred_element_type=jnp.float32).astype(jnp.bfloat16),
        "tp",
        scatter_dimension=0,
        tiled=True,
    )
    expert_out = summed.reshape(share, experts, width_model)
    back = lax.all_to_all(expert_out, "ep", split_axis=1, concat_axis=1, tiled=True)
    returned = lax.all_gather(back, "tp", axis=0, tiled=True)
    returned = returned.reshape(capacity * experts, width_model)
    first_rows = jnp.take(returned, place[:, 0], axis=0).astype(jnp.float32)
    second_rows = jnp.take(returned, place[:, 1], axis=0).astype(jnp.float32)
    combined = weight_first[:, None] * first_rows + weight_second[:, None] * second_rows
    return (combined * keep_mask.astype(jnp.float32) * 1.25).astype(jnp.bfloat16)


def solution(mesh):
    return jax.shard_map(
        shards,
        mesh=mesh,
        in_specs=(
            P("ep", None),
            P("ep", None),
            P(),
            P("ep", None, "tp"),
            P("ep", None, "tp"),
            P("ep", "tp", None),
            P("ep", None),
        ),
        out_specs=P("ep", None),
        check_vma=False,
    )
```

profile of v0, /device:TPU:0, one launch (start us, length us, event | category | flops | bytes accessed | tf_op | source)
XLA Modules:
  0.0 282.0 jit_solution(14242153663635588185)
XLA Ops:
  6.5 0.0 copy-start
  6.5 0.0 reduce-scatter.2.cloned.1.call-start
  6.5 0.9 copy.59
  7.4 0.1 eq.60
  7.6 0.1 eq.56
  7.7 1.2 reduce-window.6
  9.0 0.1 slice.34
  9.0 0.1 copy.61
  9.2 0.1 copy.62
  9.3 0.1 add_bitcast_fusion
  9.4 0.1 mul.50
  9.6 0.2 slice_reduce_fusion.1
  9.7 0.0 copy-start.2
  9.7 0.0 copy-start.4
  9.8 0.6 copy-done.2
  10.3 0.0 copy-done.4
  10.3 0.0 copy-done
  10.3 3.5 %convolution_convert_fusion = bf16[384,6144]{1,0:T(8,128)(2,1)} fusion(bf16[128,6144]{1,0:T(8,128)(2,1)S(1)} %copy-done, s32[128]{0:T(128)S(1)} %get-tuple-element.7, s32[128]{0:T(128)S(1)} %get-tuple-element.6), kind=kOutput, calls=%fused_computation.10 | convolution fusion | flops 606486528 | bytes 6292480 | tf_op jit(solution)/shard_map/dot_general | solution.py:29
  13.8 7.6 %reshape.51 = bf16[96,4,6144]{2,1,0:T(4,128)(2,1)} reshape(bf16[384,6144]{1,0:T(8,128)(2,1)} %convolution_convert_fusion) | data formatting | bytes 9437184 | tf_op jit(solution)/shard_map/reshape | solution.py:30
  21.4 4.9 %copy.64 = bf16[96,4,6144]{2,0,1:T(8,128)(2,1)S(1)} copy(bf16[96,4,6144]{2,1,0:T(4,128)(2,1)} %reshape.51) | data formatting | bytes 9437184 | tf_op jit(solution)/shard_map/reshape | solution.py:30
  26.3 58.5 %all_to_all.10 = bf16[96,4,6144]{2,0,1:T(8,128)(2,1)S(1)} all-to-all(bf16[96,4,6144]{2,0,1:T(8,128)(2,1)S(1)} %copy.64), channel_id=1, replica_groups=mesh['ep'=4,'tp'=8] {'ep'}, dimensions={1} | all-to-all | bytes 9437184 | tf_op jit(solution)/shard_map/all_to_all | solution.py:34
  84.8 5.8 %copy.65 = bf16[96,4,6144]{2,1,0:T(4,128)(2,1)} copy(bf16[96,4,6144]{2,0,1:T(8,128)(2,1)S(1)} %all_to_all.10) | data formatting | bytes 9437184 | tf_op jit(solution)/shard_map/all_to_all | solution.py:34
  90.6 7.2 %reshape.52 = bf16[384,6144]{1,0:T(8,128)(2,1)} reshape(bf16[96,4,6144]{2,1,0:T(4,128)(2,1)} %copy.65) | data formatting | bytes 9437184 | tf_op jit(solution)/shard_map/reshape | solution.py:35
  97.8 9.6 %fusion.4 = f32[384,1024]{1,0:T(8,128)S(1)} fusion(bf16[384,6144]{1,0:T(8,128)(2,1)} %reshape.52, bf16[1,6144,1024]{2,1,0:T(8,128)(2,1)} %param.12), kind=kOutput, calls=%fused_computation.7 | convolution fusion | flops 4831838208 | bytes 18874368 | tf_op jit(solution)/shard_map/dot_general | solution.py:36
  107.3 21.7 %fusion.6 = bf16[384,6144]{1,0:T(8,128)(2,1)} fusion(bf16[1,1024,6144]{2,1,0:T(8,128)(2,1)} %param.14, f32[384,1024]{1,0:T(8,128)S(1)} %fusion.4, bf16[384,6144]{1,0:T(8,128)(2,1)} %reshape.52, bf16[1,6144,1024]{2,1,0:T(8,128)(2,1)} %param.13), kind=kOutput, calls=%fused_computation.9 | convolution fusion | flops 9668395008 | bytes 36175872 | tf_op jit(solution)/shard_map/dot_general | solution.py:40
  129.0 0.0 reduce-scatter.2.cloned.1.call-update
  129.0 0.0 copy-start.6
  129.1 0.0 copy-start.1
  129.1 0.0 all-gather.2.cloned.1.call-start
  129.1 54.7 %reduce-scatter.2.cloned.1.call-done = bf16[48,6144]{1,0:T(8,128)(2,1)} async-done(((bf16[384,6144]{1,0:T(8,128)(2,1)}), bf16[48,6144]{1,0:T(8,128)(2,1)}) %reduce-scatter.2.cloned.1.call-update) | async-done | bytes 589840 | tf_op jit(solution)/shard_map/reduce_scatter | solution.py:39
  183.8 1.3 reshape.53
  185.1 0.3 copy.66
  185.4 12.9 %all_to_all.11 = bf16[12,4,6144]{2,0,1:T(8,128)(2,1)S(1)} all-to-all(bf16[12,4,6144]{2,0,1:T(8,128)(2,1)S(1)} %copy.66), channel_id=1, replica_groups=mesh['ep'=4,'tp'=8] {'ep'}, dimensions={1} | all-to-all | bytes 1179648 | tf_op jit(solution)/shard_map/all_to_all | solution.py:46
  198.3 1.3 copy.67
  199.6 0.0 all-gather.2.cloned.1.call-update
  199.6 0.0 copy-done.6
  199.6 0.1 copy.57
  199.7 0.1 reshape.71
  199.9 0.0 copy-done.1
  199.9 0.5 fusion.22
  200.4 0.0 copy-start.3
  200.4 0.0 copy-start.5
  200.4 2.4 gather_fusion
  202.8 0.1 reshape.74
  202.9 0.1 copy.58
  203.0 0.0 copy-done.3
  203.0 0.0 copy-done.5
  203.1 46.7 %all-gather.2.cloned.1.call-done = bf16[96,4,6144]{2,1,0:T(4,128)(2,1)} async-done(((bf16[12,4,6144]{2,1,0:T(4,128)(2,1)}), bf16[96,4,6144]{2,1,0:T(4,128)(2,1)}) %all-gather.2.cloned.1.call-update) | async-done | bytes 4718608 | tf_op jit(solution)/shard_map/all_gather | solution.py:47
  249.9 7.2 %reshape.54 = bf16[384,6144]{1,0:T(8,128)(2,1)} reshape(bf16[96,4,6144]{2,1,0:T(4,128)(2,1)} %all-gather.2.cloned.1.call-done) | data formatting | bytes 9437184 | tf_op jit(solution)/shard_map/reshape | solution.py:48
  257.1 5.9 %gather_fusion.1 = bf16[128,6144]{1,0:T(8,128)(2,1)S(1)} fusion(bf16[384,6144]{1,0:T(8,128)(2,1)} %reshape.54, s32[1024]{0:T(1024)S(1)} %pad_clamp_fusion.1), kind=kCustom, calls=%fused_computation.clone | custom fusion | bytes 3146240 | tf_op jit(solution)/shard_map/jit(_take)/gather | solution.py:49
  263.1 7.1 %gather_fusion.2 = bf16[128,6144]{1,0:T(8,128)(2,1)} fusion(bf16[384,6144]{1,0:T(8,128)(2,1)} %reshape.54, s32[1024]{0:T(1024)S(1)} %pad_clamp_fusion), kind=kCustom, calls=%fused_computation.1.clone | custom fusion | bytes 3146240 | tf_op jit(solution)/shard_map/jit(_take)/gather | solution.py:50
  270.2 5.0 %multiply_convert_fusion = bf16[128,6144]{1,0:T(8,128)(2,1)} fusion(s32[128,6144]{1,0:T(8,128)} %param.15, bf16[128,6144]{1,0:T(8,128)(2,1)} %gather_fusion.2, bf16[128,6144]{1,0:T(8,128)(2,1)S(1)} %gather_fusion.1, f32[128]{0:T(128)S(1)} %get-tuple-element.9, f32[128]{0:T(128)S(1)} %get-tuple-element.8, pred[128]{0:T(512)(128)(4,1)S(1)} %get-tuple-element.12, ...), kind=kLoop, calls=%fused_computation.11 | loop fusion | flops 8650752 | bytes 7865600 | tf_op jit(solution)/shard_map/convert_element_type | solution.py:52
  (13 shorter events, 0.1 us)
Async XLA Ops:
  6.5 3.8 %copy-start = (bf16[128,6144]{1,0:T(8,128)(2,1)S(1)}, bf16[128,6144]{1,0:T(8,128)(2,1)}, u32[]{:S(2)}) copy-start(bf16[128,6144]{1,0:T(8,128)(2,1)} %param.9) | copy-start | bytes 4718596
  6.5 177.2 %reduce-scatter.2.cloned.1.call-start = ((), (), s32[]{:S(2)}) async-start(), calls=%async_computation.3 | async-start | bytes 5308416 | tf_op jit(solution)/shard_map/reduce_scatter | solution.py:39
  9.7 0.6 copy-start.2
  9.7 0.6 copy-start.4
  129.0 70.6 %copy-start.6 = (s32[128,2]{0,1:T(2,128)S(1)}, s32[128,2]{0,1:T(2,128)}, u32[]{:S(2)}) copy-start(s32[128,2]{0,1:T(2,128)} %param.10) | copy-start | bytes 3076
  129.1 70.8 %copy-start.1 = (bf16[6144,4]{0,1:T(4,128)(2,1)S(1)}, bf16[6144,4]{0,1:T(4,128)(2,1)}, u32[]{:S(2)}) copy-start(bf16[6144,4]{0,1:T(4,128)(2,1)} %param.11) | copy-start | bytes 147460
  129.1 120.8 %all-gather.2.cloned.1.call-start = ((), (), s32[]{:S(2)}) async-start(), calls=%async_computation.4 | async-start | bytes 5308416 | tf_op jit(solution)/shard_map/all_gather | solution.py:47
  200.4 2.6 copy-start.3
  200.4 2.6 copy-start.5
Sparse Core Ops, SparseCore 0:
  129.2 54.5 reduce-scatter.1
  199.7 50.0 all-gather.1
where the time goes:
time: 283 us; the launch traced here: 282 us
  waiting for transfers between devices  101 us (36%)
  blocking collectives  71.4 us (25%)
  local copies, waits for them, and re-layouts  53.9 us (19%)
  matrix products  35.2 us (12%)
  between operations  13.6 us (5%)
  other arithmetic  6.43 us (2%)
    all_to_all x1, blocking collectives, shards(): lax.all_to_all(outgoing, 'ep', split_axis=1, concat_axis=1, tiled=True)  58.5 us
    reduce_scatter x1, waiting for transfers between devices, shards(): lax.psum_scatter(jnp.dot(hidden, w_down, preferred_element_type=jnp.float...  54.7 us
    all_gather x1, waiting for transfers between devices, shards(): returned = lax.all_gather(back, 'tp', axis=0, tiled=True)  46.7 us
    dot_general x1, matrix products, shards(): jnp.dot(hidden, w_down, preferred_element_type=jnp.float32)  21.7 us
    all_to_all x1, blocking collectives, shards(): lax.all_to_all(expert_out, 'ep', split_axis=1, concat_axis=1, tiled=True)  12.9 us
    reshape x2, local copies, waits for them, and re-layouts, shards(): outgoing = outgoing.reshape(capacity, experts, width_model)  12.5 us
    dot_general x1, matrix products, shards(): gate = jnp.dot(rows, w_gate, preferred_element_type=jnp.float32)  9.55 us
    reshape x1, local copies, waits for them, and re-layouts, shards(): returned = returned.reshape(capacity * experts, width_model)  7.25 us
  transfers between devices with their start and end apart: 2, of which 2 were waited for; matrix products, arithmetic and copies ran while one was open for 1% of the time, Pallas kernels for 0%

commit v1 on v0

--- a/solution.py
+++ b/solution.py
@@ -31,7 +31,10 @@
     w_gate = gate_weight[0]
     w_up = up_weight[0]
     w_down = down_weight[0]
-    arrived = lax.all_to_all(outgoing, "ep", split_axis=1, concat_axis=1, tiled=True)
+    arrived = jnp.concatenate(
+        lax.all_to_all(jnp.stack(jnp.split(outgoing, lax.axis_size("ep"), axis=1)), "ep", 0, 0),
+        axis=1,
+    )
     rows = arrived.reshape(capacity * experts, width_model)
     gate = jnp.dot(rows, w_gate, preferred_element_type=jnp.float32)
     up = jnp.dot(rows, w_up, preferred_element_type=jnp.float32)

time: 283 us -> 297 us (1.049)
  local copies, waits for them, and re-layouts: 53.9 us -> 67.2 us
    split x0 -> x1, local copies, waits for them, and re-layouts: none -> 15.5 us  [shards(): jnp.split(outgoing, lax.axis_size('ep'), axis=1)]
    another operation x2 -> x5, local copies, waits for them, and re-layouts: 0.1 us -> 9.97 us  [the longest x1 7.22 us: shards(): rows = arrived.reshape(capacity * experts, width_model)]
    all_to_all x1 -> x0, local copies, waits for them, and re-layouts: 5.81 us -> none  [shards(): lax.all_to_all(outgoing, 'ep', split_axis=1, concat_axis=1, tiled=True)]
    reshape x2 -> x1, local copies, waits for them, and re-layouts: 12.5 us -> 7.59 us  [shards(): outgoing = outgoing.reshape(capacity, experts, width_model)]
where the time goes in v1:
time: 297 us; the launch traced here: 296 us
  waiting for transfers between devices  102 us (34%)
  blocking collectives  71.3 us (24%)
  local copies, waits for them, and re-layouts  67.2 us (23%)
  matrix products  35.3 us (12%)
  between operations  13.6 us (5%)
  other arithmetic  7.07 us (2%)
    all_to_all x1, blocking collectives, shards(): lax.all_to_all(jnp.stack(jnp.split(outgoing, lax.axis_size('ep'), axis=1)...  58.5 us
    reduce_scatter x1, waiting for transfers between devices, shards(): lax.psum_scatter(jnp.dot(hidden, w_down, preferred_element_type=jnp.float...  54.7 us
    all_gather x1, waiting for transfers between devices, shards(): returned = lax.all_gather(back, 'tp', axis=0, tiled=True)  46.8 us
    dot_general x1, matrix products, shards(): jnp.dot(hidden, w_down, preferred_element_type=jnp.float32)  21.7 us
    split x1, local copies, waits for them, and re-layouts, shards(): jnp.split(outgoing, lax.axis_size('ep'), axis=1)  15.5 us
    all_to_all x1, blocking collectives, shards(): lax.all_to_all(expert_out, 'ep', split_axis=1, concat_axis=1, tiled=True)  12.9 us
    dot_general x1, matrix products, shards(): gate = jnp.dot(rows, w_gate, preferred_element_type=jnp.float32)  9.59 us
    reshape x1, local copies, waits for them, and re-layouts, shards(): outgoing = outgoing.reshape(capacity, experts, width_model)  7.59 us
  transfers between devices with their start and end apart: 2, of which 2 were waited for; matrix products, arithmetic and copies ran while one was open for 1% of the time, Pallas kernels for 0%

profile of v1, /device:TPU:0, one launch (start us, length us, event | category | flops | bytes accessed | tf_op | source)
XLA Modules:
  0.0 296.0 jit_solution(806544178255644599)
XLA Ops:
  6.5 0.0 copy-start
  6.5 0.0 reduce-scatter.2.cloned.1.call-start
  6.5 0.9 copy.62
  7.4 0.1 eq.60
  7.6 0.1 eq.56
  7.7 1.2 reduce-window.6
  9.0 0.1 slice.34
  9.0 0.1 copy.64
  9.2 0.1 copy.65
  9.3 0.1 add_bitcast_fusion
  9.4 0.1 mul.50
  9.6 0.2 slice_reduce_fusion.1
  9.7 0.0 copy-start.2
  9.7 0.0 copy-start.4
  9.8 0.6 copy-done.2
  10.3 0.0 copy-done.4
  10.3 0.0 copy-done
  10.3 3.5 %convolution_convert_fusion = bf16[384,6144]{1,0:T(8,128)(2,1)} fusion(bf16[128,6144]{1,0:T(8,128)(2,1)S(1)} %copy-done, s32[128]{0:T(128)S(1)} %get-tuple-element.7, s32[128]{0:T(128)S(1)} %get-tuple-element.6), kind=kOutput, calls=%fused_computation.10 | convolution fusion | flops 606486528 | bytes 6292480 | tf_op jit(solution)/shard_map/dot_general | solution.py:29
  13.8 7.6 %reshape.51 = bf16[96,4,6144]{2,1,0:T(4,128)(2,1)} reshape(bf16[384,6144]{1,0:T(8,128)(2,1)} %convolution_convert_fusion) | data formatting | bytes 9437184 | tf_op jit(solution)/shard_map/reshape | solution.py:30
  21.4 15.5 %fusion.22 = (bf16[96,1,6144]{2,1,0:T(2,128)(2,1)S(1)}, bf16[96,1,6144]{2,1,0:T(2,128)(2,1)S(1)}, bf16[96,1,6144]{2,1,0:T(2,128)(2,1)S(1)}, bf16[96,1,6144]{2,1,0:T(2,128)(2,1)S(1)}) fusion(bf16[96,4,6144]{2,1,0:T(4,128)(2,1)} %reshape.51), kind=kLoop, calls=%fused_computation.46 | loop fusion | bytes 9437184 | tf_op jit(solution)/shard_map/split | solution.py:35
  36.9 1.3 copy_bitcast_fusion.2
  38.2 1.3 copy_bitcast_fusion
  39.6 0.6 pad_maximum_fusion
  40.2 58.5 %all_to_all.10 = bf16[4,96,1,6144]{3,1,2,0:T(8,128)(2,1)S(1)} all-to-all(bf16[4,96,1,6144]{3,1,2,0:T(8,128)(2,1)S(1)} %pad_maximum_fusion), channel_id=1, replica_groups=mesh['ep'=4,'tp'=8] {'ep'}, dimensions={0} | all-to-all | bytes 9437184 | tf_op jit(solution)/shard_map/all_to_all | solution.py:35
  98.7 5.8 %copy.71 = bf16[96,4,1,6144]{3,1,0,2:T(4,128)(2,1)} copy(bf16[96,4,1,6144]{3,0,2,1:T(8,128)(2,1)S(1)} %bitcast.58) | data formatting | bytes 9437184 | tf_op jit(solution)/shard_map/reshape | solution.py:34
  104.5 7.2 %reshape_reshape.3 = bf16[384,6144]{1,0:T(8,128)(2,1)} reshape(bf16[96,4,1,6144]{3,1,0,2:T(4,128)(2,1)} %copy.71) | data formatting | bytes 9437184 | tf_op jit(solution)/shard_map/reshape;reshape | solution.py:38
  111.7 9.6 %fusion.4 = f32[384,1024]{1,0:T(8,128)S(1)} fusion(bf16[384,6144]{1,0:T(8,128)(2,1)} %reshape_reshape.3, bf16[1,6144,1024]{2,1,0:T(8,128)(2,1)} %param.12), kind=kOutput, calls=%fused_computation.7 | convolution fusion | flops 4831838208 | bytes 18874368 | tf_op jit(solution)/shard_map/dot_general | solution.py:39
  121.3 21.7 %fusion.6 = bf16[384,6144]{1,0:T(8,128)(2,1)} fusion(bf16[1,1024,6144]{2,1,0:T(8,128)(2,1)} %param.14, f32[384,1024]{1,0:T(8,128)S(1)} %fusion.4, bf16[384,6144]{1,0:T(8,128)(2,1)} %reshape_reshape.3, bf16[1,6144,1024]{2,1,0:T(8,128)(2,1)} %param.13), kind=kOutput, calls=%fused_computation.9 | convolution fusion | flops 9668395008 | bytes 36175872 | tf_op jit(solution)/shard_map/dot_general | solution.py:43
  143.0 0.0 reduce-scatter.2.cloned.1.call-update
  143.0 0.0 all-gather.2.cloned.1.call-start
  143.0 54.7 %reduce-scatter.2.cloned.1.call-done = bf16[48,6144]{1,0:T(8,128)(2,1)} async-done(((bf16[384,6144]{1,0:T(8,128)(2,1)}), bf16[48,6144]{1,0:T(8,128)(2,1)}) %reduce-scatter.2.cloned.1.call-update) | async-done | bytes 589840 | tf_op jit(solution)/shard_map/reduce_scatter | solution.py:42
  197.8 1.3 reshape.53
  199.0 0.0 copy-start.6
  199.1 0.0 copy-start.1
  199.1 0.3 copy.72
  199.4 12.9 %all_to_all.11 = bf16[12,4,6144]{2,0,1:T(8,128)(2,1)S(1)} all-to-all(bf16[12,4,6144]{2,0,1:T(8,128)(2,1)S(1)} %copy.72), channel_id=1, replica_groups=mesh['ep'=4,'tp'=8] {'ep'}, dimensions={1} | all-to-all | bytes 1179648 | tf_op jit(solution)/shard_map/all_to_all | solution.py:49
  212.3 1.3 copy.73
  213.6 0.0 all-gather.2.cloned.1.call-update
  213.6 0.0 copy-done.6
  213.6 0.1 copy.60
  213.7 0.1 reshape.71
  213.9 0.0 copy-done.1
  213.9 0.5 fusion.23
  214.4 0.0 copy-start.3
  214.4 0.0 copy-start.5
  214.4 2.4 gather_fusion
  216.8 0.1 reshape.74
  216.9 0.1 copy.61
  217.0 0.0 copy-done.3
  217.0 0.0 copy-done.5
  217.1 46.8 %all-gather.2.cloned.1.call-done = bf16[96,4,6144]{2,1,0:T(4,128)(2,1)} async-done(((bf16[12,4,6144]{2,1,0:T(4,128)(2,1)}), bf16[96,4,6144]{2,1,0:T(4,128)(2,1)}) %all-gather.2.cloned.1.call-update) | async-done | bytes 4718608 | tf_op jit(solution)/shard_map/all_gather | solution.py:50
  263.9 7.3 %reshape.54 = bf16[384,6144]{1,0:T(8,128)(2,1)} reshape(bf16[96,4,6144]{2,1,0:T(4,128)(2,1)} %all-gather.2.cloned.1.call-done) | data formatting | bytes 9437184 | tf_op jit(solution)/shard_map/reshape | solution.py:51
  271.1 5.9 %gather_fusion.1 = bf16[128,6144]{1,0:T(8,128)(2,1)S(1)} fusion(bf16[384,6144]{1,0:T(8,128)(2,1)} %reshape.54, s32[1024]{0:T(1024)S(1)} %pad_clamp_fusion.1), kind=kCustom, calls=%fused_computation.clone | custom fusion | bytes 3146240 | tf_op jit(solution)/shard_map/jit(_take)/gather | solution.py:52
  277.1 7.1 %gather_fusion.2 = bf16[128,6144]{1,0:T(8,128)(2,1)} fusion(bf16[384,6144]{1,0:T(8,128)(2,1)} %reshape.54, s32[1024]{0:T(1024)S(1)} %pad_clamp_fusion), kind=kCustom, calls=%fused_computation.1.clone | custom fusion | bytes 3146240 | tf_op jit(solution)/shard_map/jit(_take)/gather | solution.py:53
  284.1 5.0 %multiply_convert_fusion = bf16[128,6144]{1,0:T(8,128)(2,1)} fusion(s32[128,6144]{1,0:T(8,128)} %param.15, bf16[128,6144]{1,0:T(8,128)(2,1)} %gather_fusion.2, bf16[128,6144]{1,0:T(8,128)(2,1)S(1)} %gather_fusion.1, f32[128]{0:T(128)S(1)} %get-tuple-element.13, f32[128]{0:T(128)S(1)} %get-tuple-element.12, pred[128]{0:T(512)(128)(4,1)S(1)} %get-tuple-element.16, ...), kind=kLoop, calls=%fused_computation.12 | loop fusion | flops 8650752 | bytes 7865600 | tf_op jit(solution)/shard_map/convert_element_type | solution.py:55
  (13 shorter events, 0.1 us)
Async XLA Ops:
  6.5 3.8 %copy-start = (bf16[128,6144]{1,0:T(8,128)(2,1)S(1)}, bf16[128,6144]{1,0:T(8,128)(2,1)}, u32[]{:S(2)}) copy-start(bf16[128,6144]{1,0:T(8,128)(2,1)} %param.9) | copy-start | bytes 4718596
  6.5 191.2 %reduce-scatter.2.cloned.1.call-start = ((), (), s32[]{:S(2)}) async-start(), calls=%async_computation.3 | async-start | bytes 5308416 | tf_op jit(solution)/shard_map/reduce_scatter | solution.py:42
  9.7 0.6 copy-start.2
  9.7 0.6 copy-start.4
  143.0 120.9 %all-gather.2.cloned.1.call-start = ((), (), s32[]{:S(2)}) async-start(), calls=%async_computation.4 | async-start | bytes 5308416 | tf_op jit(solution)/shard_map/all_gather | solution.py:50
  199.0 14.5 %copy-start.6 = (s32[128,2]{0,1:T(2,128)S(1)}, s32[128,2]{0,1:T(2,128)}, u32[]{:S(2)}) copy-start(s32[128,2]{0,1:T(2,128)} %param.10) | copy-start | bytes 3076
  199.1 14.8 %copy-start.1 = (bf16[6144,4]{0,1:T(4,128)(2,1)S(1)}, bf16[6144,4]{0,1:T(4,128)(2,1)}, u32[]{:S(2)}) copy-start(bf16[6144,4]{0,1:T(4,128)(2,1)} %param.11) | copy-start | bytes 147460
  214.4 2.6 copy-start.3
  214.4 2.6 copy-start.5
Sparse Core Ops, SparseCore 0:
  143.1 54.5 reduce-scatter.1
  213.7 50.0 all-gather.1
